TPU v7x, 128 devices: a whole 4x4x4 slice. The times are simulated.
128 devices in a mesh: data: 1, cp: 128 (over z, y, x, core).
Axes of the slice: x: 4, y: 4, z: 4, core: 2. Of those that a mesh axis runs over, the one named last changes fastest.
Arguments:
- x_new: bfloat16 [4096, 5120], P(('data', 'cp'))
- pos_new: int32 [4096], P(('data', 'cp'))
- k_cache: bfloat16 [32768, 8, 128], P(('data', 'cp'))
- v_cache: bfloat16 [32768, 8, 128], P(('data', 'cp'))
- w_q: bfloat16 [5120, 4096], replicated
- w_k: bfloat16 [5120, 1024], replicated
- w_v: bfloat16 [5120, 1024], replicated
- w_o: bfloat16 [4096, 5120], replicated
Outputs:
- output: bfloat16 [4096, 5120], P(('data', 'cp'))
All inputs are finite; a program needn't handle non-finite values.
Results may differ from a plain program's by a relative error of at most 0.00547.
Values are sent between devices in bfloat16 or wider.
A program may use at most 1 GiB of HBM per device.

v0:
```python
import math
import jax
import jax.numpy as jnp
from jax import lax
from jax.sharding import PartitionSpec as P

ROPE_BASE = 500000.0
SCORE_BUDGET = 2 ** 26


def rotary(values, positions):
    head_dim = values.shape[-1]
    half_dim = head_dim // 2
    inv_freq = jnp.power(jnp.float32(ROPE_BASE), -(jnp.arange(half_dim, dtype=jnp.float32) * 2.0 / head_dim))
    angles = positions.astype(jnp.float32)[:, None] * inv_freq[None, :]
    cos_a = jnp.cos(angles)[:, None, :]
    sin_a = jnp.sin(angles)[:, None, :]
    low_half = values[..., :half_dim]
    high_half = values[..., half_dim:]
    return jnp.concatenate([low_half * cos_a - high_half * sin_a, high_half * cos_a + low_half * sin_a], axis=-1)


def block_rows(tok_count, row_bytes):
    blk_rows = tok_count
    while blk_rows % 2 == 0 and blk_rows > 8 and blk_rows * row_bytes > SCORE_BUDGET:
        blk_rows = blk_rows // 2
    return blk_rows


def solution(mesh):
    cp_size = mesh.shape["cp"]

    def local_step(x_loc, pos_loc, k_loc, v_loc, w_q, w_k, w_v, w_o):
        tok_dev, model_dim = x_loc.shape
        cache_dev, kv_heads, head_dim = k_loc.shape
        q_heads = w_q.shape[1] // head_dim
        group_size = q_heads // kv_heads
        score_scale = 1.0 / math.sqrt(head_dim)
        q_proj = jnp.dot(x_loc, w_q, preferred_element_type=jnp.float32).astype(jnp.bfloat16)
        k_proj = jnp.dot(x_loc, w_k, preferred_element_type=jnp.float32).astype(jnp.bfloat16)
        v_new = jnp.dot(x_loc, w_v, preferred_element_type=jnp.float32).astype(jnp.bfloat16).reshape(tok_dev, kv_heads, head_dim)
        q_rot = rotary(q_proj.astype(jnp.float32).reshape(tok_dev, q_heads, head_dim), pos_loc).astype(jnp.bfloat16)
        k_new = rotary(k_proj.astype(jnp.float32).reshape(tok_dev, kv_heads, head_dim), pos_loc).astype(jnp.bfloat16)
        keys_all = jnp.concatenate([k_loc, k_new], axis=0)
        vals_all = jnp.concatenate([v_loc, v_new], axis=0)
        key_pos = jnp.concatenate([jnp.full((cache_dev,), -1, jnp.int32), pos_loc])
        q_all = lax.all_gather(q_rot, "cp", axis=0, tiled=True)
        pos_all = lax.all_gather(pos_loc, "cp", axis=0, tiled=True)
        blk_rows = block_rows(tok_dev, q_heads * (cache_dev + tok_dev) * 4)
        n_sub = tok_dev // blk_rows
        q_blocks = q_all.reshape(cp_size * n_sub, blk_rows, kv_heads, group_size, head_dim)
        pos_blocks = pos_all.reshape(cp_size * n_sub, blk_rows)

        def attend(block_args):
            q_blk, q_pos = block_args
            scores = jnp.einsum("qkgd,ckd->kqgc", q_blk, keys_all, preferred_element_type=jnp.float32) * score_scale
            visible = key_pos[None, :] <= q_pos[:, None]
            scores = jnp.where(visible[None, :, None, :], scores, -jnp.inf)
            row_max = jnp.max(scores, axis=-1)
            exp_scores = jnp.exp(scores - row_max[..., None])
            row_sum = jnp.sum(exp_scores, axis=-1)
            weighted = jnp.einsum("kqgc,ckd->kqgd", exp_scores.astype(jnp.bfloat16), vals_all, preferred_element_type=jnp.float32)
            return jnp.stack([row_max, row_sum], axis=-1), weighted

        stats, weighted = lax.map(attend, (q_blocks, pos_blocks))
        stats = stats.reshape(cp_size, n_sub, kv_heads, blk_rows, group_size, 2)
        weighted = weighted.reshape(cp_size, n_sub, kv_heads, blk_rows, group_size, head_dim)
        stats = lax.all_to_all(stats, "cp", 0, 0)
        weighted = lax.all_to_all(weighted, "cp", 0, 0)
        glob_max = jnp.max(stats[..., 0], axis=0)
        factors = jnp.exp(stats[..., 0] - glob_max[None])
        denom_sum = jnp.sum(factors * stats[..., 1], axis=0)
        attn_out = (jnp.sum(factors[..., None] * weighted, axis=0) / denom_sum[..., None]).astype(jnp.bfloat16)
        w_out = w_o.reshape(kv_heads, group_size, head_dim, model_dim)
        proj_out = jnp.einsum("skrgd,kgde->sre", attn_out, w_out, preferred_element_type=jnp.float32).reshape(tok_dev, model_dim)
        return (x_loc.astype(jnp.float32) + proj_out).astype(jnp.bfloat16)

    tok_spec = P(("data", "cp"), None)
    pos_spec = P(("data", "cp"))
    cache_spec = P(("data", "cp"), None, None)
    return jax.shard_map(local_step, mesh=mesh, in_specs=(tok_spec, pos_spec, cache_spec, cache_spec, P(), P(), P(), P()), out_specs=tok_spec, check_vma=False)
```

profile of v0, /device:TPU:117, one launch (start us, length us, event | category | flops | bytes accessed | tf_op | source)
XLA Modules:
  0.0 1886.2 jit_solution(17614699728370484138)
XLA Ops:
  7.2 16.7 fusion.29
  26.0 6.0 fusion.31
  32.9 1.9 fusion.32
  35.1 63.1 %all-reduce.1 = s32[4096]{0:T(1024)S(1)} all-reduce(s32[4096]{0:T(1024)S(1)} %dynamic-update-slice), channel_id=1, replica_groups=mesh['data'=1,'cp'=128] {'cp'}, use_global_device_ids=true, to_apply=%add.1 | all-reduce | flops 4096 | bytes 32768
  99.6 50.1 %all-gather.2.cloned.1.call-done = bf16[4096,32,128]{2,0,1:T(8,128)(2,1)} async-done(((bf16[32,32,128]{2,0,1:T(8,128)(2,1)}), bf16[4096,32,128]{2,0,1:T(8,128)(2,1)}) %all-gather.2.cloned.1.call-update) | async-done | bytes 33554448 | tf_op jit(solution)/shard_map/all_gather | solution.py:47
  149.7 506.3 %while.12 = (s32[]{:T(128)}, f32[128,8,32,4,2]{2,3,1,4,0:T(4,128)}, f32[128,8,32,4,128]{4,2,3,1,0:T(8,128)}, s32[288]{0:T(512)S(1)}, s32[128,32]{1,0:T(8,128)S(1...) while((s32[]{:T(128)}, f32[128,8,32,4,2]{2,3,1,4,0:T(4,128)}, ...), condition=%wide.region_3.4_spmd, body=%wide.region_0.3_spmd.sunk | while | flops 153068544 | bytes 5583969 | solution.py:65
  165.6 1.4 fusion.53
  177.4 1.4 fusion.53
  193.3 1.4 fusion.53
  213.1 1.4 fusion.53
  221.1 1.4 fusion.53
  272.4 1.4 fusion.53
  288.2 1.4 fusion.53
  656.0 6.0 bitcast_bitcast_fusion
  662.0 4.3 reshape.187
  666.3 23.2 %all_to_all.10 = f32[128,1,2048]{2,1,0:T(1,128)S(1)} all-to-all(f32[128,1,2048]{2,1,0:T(1,128)S(1)} %reshape.187), channel_id=1, replica_groups=mesh['data'=1,'cp'=128] {'cp'}, dimensions={0} | all-to-all | bytes 2097152 | tf_op jit(solution)/shard_map/all_to_all | solution.py:68
  689.6 12.8 all-to-all-start.1
  702.8 3.1 reduce.4
  706.0 3.5 reshape.188
  709.5 2.2 bitcast_reduce_fusion.1
  711.7 3.3 fusion.25
  715.6 1125.7 %all-to-all-done.1 = f32[128,1,8,32,4,128]{5,3,4,2,1,0:T(8,128)} async-done(((f32[128,1,8,32,4,128]{5,3,4,2,1,0:T(8,128)}), f32[128,1,8,32,4,128]{5,3,4,2,1,0:T(8,128)}, u32[]{:S(2)}, u32[]{:S(2)}) %all-to-all-start.1) | async-done | bytes 67108896 | tf_op jit(solution)/shard_map/all_to_all | solution.py:69
  1841.3 22.1 %bitcast_reduce_fusion = f32[8,32,4,128]{3,1,2,0:T(8,128)S(1)} fusion(f32[128,1,8,32,4,128]{5,3,4,2,1,0:T(8,128)} %all-to-all-done.1, f32[128,8,32,4]{2,3,1,0:T(4,128)S(1)} %fusion.28), kind=kLoop, calls=%fused_computation.17 | loop fusion | flops 33423360 | bytes 68157440 | tf_op jit(solution)/shard_map/reduce_sum | solution.py:73
  1863.4 15.9 fusion.20
  (802 shorter events, 501.3 us)
Async XLA Ops:
  6.5 143.2 %all-gather.2.cloned.1.call-start = ((), (), s32[]{:S(2)}) async-start(), calls=%async_computation.2 | async-start | bytes 33816576 | tf_op jit(solution)/shard_map/all_gather | solution.py:47
  23.9 2.0 copy-start.1
  25.0 7.9 slice-start
  26.0 6.8 copy-start.2
  26.0 6.8 copy-start.3
  26.0 6.9 slice-start.1
  26.0 6.9 slice-start.2
  32.9 2.0 copy-start.4
  689.6 1151.7 %all-to-all-start.1 = ((f32[128,1,8,32,4,128]{5,3,4,2,1,0:T(8,128)}), f32[128,1,8,32,4,128]{5,3,4,2,1,0:T(8,128)}, u32[]{:S(2)}, u32[]{:S(2)}) async-start(f32[128,1,8,32,4,128]{5,3,4,2,1,0:T(8,128)} %bitcast.13), calls=%async_computation.1 | async-start | bytes 134217728 | tf_op jit(solution)/shard_map/all_to_all | solution.py:69
  709.5 5.5 copy-start
Sparse Core Ops, SparseCore 0:
  26.0 123.6 all-gather.1
where the time goes:
time: 1890 us
  waiting for transfers between devices  1180 us (62%)
  matrix products  385 us (20%)
  other arithmetic  194 us (10%)
  blocking collectives  86.4 us (5%)
    all_to_all x1, waiting for transfers between devices, local_step(): weighted = lax.all_to_all(weighted, 'cp', 0, 0)  1130 us
    dot_general x128, matrix products, attend(): jnp.einsum('qkgd,ckd->kqgc', q_blk, keys_all, preferred_element_type=jnp....  184 us
    dot_general x128, matrix products, attend(): jnp.einsum('kqgc,ckd->kqgd', exp_scores.astype(jnp.bfloat16), vals_all, p...  160 us
    dynamic_update_slice x128, other arithmetic, local_step(): stats, weighted = lax.map(attend, (q_blocks, pos_blocks))  78.8 us
    reduce_sum x128, other arithmetic, attend(): row_sum = jnp.sum(exp_scores, axis=-1)  71.5 us
    unnamed x1, blocking collectives  63.1 us
    all_gather x1, waiting for transfers between devices, local_step(): q_all = lax.all_gather(q_rot, 'cp', axis=0, tiled=True)  50.1 us
  transfers between devices with their start and end apart: 2, of which 2 were waited for; matrix products, arithmetic and copies ran while one was open for 1% of the time, Pallas kernels for 0%

commit v1 on v0

v1 whole, which is shorter than its diff:
```python
import math

import jax
import jax.numpy as jnp
from jax import lax
from jax.experimental import pallas as pl
from jax.experimental.pallas import tpu as pltpu
from jax.sharding import PartitionSpec as P

ROPE_BASE = 500000.0
F32 = jnp.float32
BF16 = jnp.bfloat16
HD = 128
SUB = 8
HEADS = 8
TOK = 32
HALF = TOK // 2
PAIR = 2 * TOK
CACHE = 256
QB = 512
KT = 2048
KN = 1024
RC = 256
SCALE2 = (1.0 / math.sqrt(HD)) * math.log2(math.e)
MODEL = 5120
GRP = 512
WCOLS = GRP + 2 * HD
QCOLS = 4096
OHALF = MODEL // 2
KSTEP = 2560
OSTEP = 2048
OTILES = (WCOLS, WCOLS, WCOLS, CACHE)
LAST_POS = 4064
PIECES = (0, 4, 1, 3, 5, 7, 2, 6)
TILES = 0xEE7DA5
BLOCKS = 0xFAD244
NEG = float(jnp.finfo(jnp.float32).min)
ACC = slice(HD)
MROW = slice(HD, HD + SUB)
LROW = slice(HD + SUB, HD + 2 * SUB)
STAT = HD + 2 * SUB
KROWS = slice(CACHE)
VLO = slice(CACHE, CACHE + HD)
VHI = slice(CACHE + HD, 2 * CACHE)


def dev(x, y, z, c):
    return ((z * 4 + y) * 4 + x) * 2 + c


def rel_pos(d, t):
    return jnp.where(t < HALF, HALF * d + t, LAST_POS - HALF * d + t)


def rcopy(src, dst, ss, rs, d):
    return pltpu.make_async_remote_copy(
        src_ref=src, dst_ref=dst, send_sem=ss, recv_sem=rs, device_id={"cp": d},
        device_id_type=pl.DeviceIdType.MESH)


def drain(ref, sem):
    pltpu.make_async_copy(ref, ref, sem).wait()


def unless(cond, run, other=None):
    pl.when(jnp.logical_not(cond))(run)
    if other is not None:
        pl.when(cond)(other)


def kernel(
    x_hbm, k_hbm, v_hbm, cos_ref, sin_ref, wq, wk, wv, wo, out_hbm,
    xbuf, kraw, kvsrc, kvt, kvn, newbuf, qbuf, qt, qsend, nsend, accs, cb_core, cb_y, sbuf,
    wbuf, osend, obuf, olhs, kpos, ysend, ybuf,
    loc_sem, w_sem, x_sem, kv1_s, kv1_r, kvx_s, kvx_r, q_s, q_r, qd_s, qd_r,
    n_s, n_r, nx_s, nx_r, cc_s, cc_r, cy_s, cy_r, o_s, o_r, od_s, od_r, y_s, y_r,
):
    me = lax.axis_index("cp")
    c = lax.rem(me, 2)
    x = lax.rem(me // 2, 4)
    y = lax.rem(me // 8, 4)
    z = me // 32
    nc = 1 - c
    half_b = y // 2
    s = lax.rem(y, 2)
    head = 2 * z + half_b
    src_core = head // 4
    here = z * 4 + y
    mate = dev(x, y, z, nc)
    xr, xl, xo = (lax.rem(x + i, 4) for i in (1, 3, 2))
    my_tok = pl.ds(pl.multiple_of(c * TOK, TOK), TOK)
    mate_tok = pl.ds(pl.multiple_of(nc * TOK, TOK), TOK)

    def wcopies(i):
        h = 4 * c + i
        cols = pl.ds(pl.multiple_of(h * HD, HD), HD)
        return [
            pltpu.make_async_copy(wq.at[:, pl.ds(pl.multiple_of(h * GRP, GRP), GRP)], wbuf.at[i, :, pl.ds(0, GRP)], w_sem.at[i]),
            pltpu.make_async_copy(wk.at[:, cols], wbuf.at[i, :, pl.ds(GRP, HD)], w_sem.at[i]),
            pltpu.make_async_copy(wv.at[:, cols], wbuf.at[i, :, pl.ds(GRP + HD, HD)], w_sem.at[i]),
        ]

    def wo_copy(n):
        wide = OTILES[n]
        cols = pl.ds(pl.multiple_of(c * OHALF, HD) + n * WCOLS, wide)
        return pltpu.make_async_copy(wo.at[:, cols], wbuf.at[n, pl.ds(0, QCOLS), pl.ds(0, wide)], w_sem.at[4 + n])

    first = [
        pltpu.make_async_copy(k_hbm, kraw.at[0], loc_sem.at[0]),
        pltpu.make_async_copy(v_hbm, kraw.at[1], loc_sem.at[1]),
        pltpu.make_async_copy(x_hbm, xbuf.at[my_tok, :], loc_sem.at[2]),
    ]
    for cp in first:
        cp.start()

    barrier = pltpu.get_barrier_semaphore()

    def greet(d):
        pl.semaphore_signal(barrier, inc=1, device_id={"cp": d}, device_id_type=pl.DeviceIdType.MESH)

    greet(mate)
    for xx in (xr, xl, xo):
        greet(dev(xx, y, z, c))

    def greet_chip(i, _):
        for cc in range(2):
            pl.when(i != here)(lambda: greet(dev(x, lax.rem(i, 4), i // 4, cc)))
        return _

    lax.fori_loop(0, 16, greet_chip, 0)

    for cp in first:
        cp.wait()
    for i in range(4):
        for cp in wcopies(i):
            cp.start()
    for hb in range(2):
        rows = slice(hb * HD, (hb + 1) * HD)
        kh = pltpu.einshape("abc->bac", kraw[0, rows])
        vh = pltpu.einshape("abc->bac", kraw[1, rows])
        for h in range(HEADS):
            kvsrc[h, rows, :] = kh[h]
            kvsrc[h, (VLO, VHI)[hb], :] = vh[h].T
    kvt[0, 0] = kvsrc[head]

    accs[:, ACC, :] = jnp.zeros((HEADS, HD, QB), F32)
    accs[:, MROW, :] = jnp.full((HEADS, SUB, QB), NEG, F32)
    accs[:, LROW, :] = jnp.zeros((HEADS, SUB, QB), F32)
    for xs in range(4):
        row = lax.broadcasted_iota(jnp.int32, (RC, HD), 0)
        r = row // TOK
        zs = lax.rem(z + lax.rem(r, 4), 4)
        ys = jnp.where(r >= 4, 3 - y, y)
        kpos[xs] = rel_pos(dev((x, xl, xr, xo)[xs], ys, zs, c), lax.rem(row, TOK))

    pl.semaphore_wait(barrier, 34)

    x_ex = rcopy(x_hbm, xbuf.at[my_tok, :], x_sem.at[0], x_sem.at[1], mate)
    x_ex.start()

    def slot(xs, p):
        return kvt.at[p // 4 * 2 + xs // 2, xs % 2 * 4 + p % 4]

    def ring_send(p):
        rcopy(slot(0, p), slot(1, p), kvx_s, kvx_r.at[1, p // 4], dev(xr, y, z, c)).start()
        rcopy(slot(0, p), slot(2, p), kvx_s, kvx_r.at[2, p // 4], dev(xl, y, z, c)).start()

    def stage1_send(p):
        r = PIECES[p]
        zd = lax.rem(z + 4 - r % 4, 4)
        yd = 3 - y if r >= 4 else y
        rcopy(kvsrc.at[2 * zd + yd // 2], slot(0, p), kv1_s, kv1_r.at[p], dev(x, yd, zd, c)).start()

    def stage1_arrive(p):
        drain(slot(0, p), kv1_r.at[p])
        ring_send(p)

    def ring_wait(xs, half):
        drain(kvt.at[0, pl.ds(0, 4)], kvx_r.at[xs, half])

    def forward(src, p):
        to = xr if src == 1 else xl
        rcopy(slot(src, p), slot(3, p), kvx_s, kvx_r.at[3, p // 4], dev(to, y, z, c)).start()

    for p in range(1, 4):
        stage1_send(p)
    ring_send(0)

    x_ex.wait_recv()

    def q_dst(i, ss, tau):
        h = 4 * c + i
        return dev(x, 2 * lax.rem(h, 2) + ss, h // 2, tau)

    def q_copy(i, ss, tau):
        return rcopy(qsend.at[i, tau], qbuf.at[tau, here], q_s, q_r.at[here // 4], q_dst(i, ss, tau))

    def n_dst(i):
        h = 4 * c + i
        zd = h // 2
        same = lax.rem(h, 2) == half_b
        return dev(x, jnp.where(same, y, 3 - y), zd, 0), jnp.where(same, 0, 4) + lax.rem(z + 4 - zd, 4)

    def n_copy(i, tau):
        d, r = n_dst(i)
        return rcopy(nsend.at[i, tau], newbuf.at[0, r], n_s, n_r, d + tau)

    cosv = jnp.concatenate([cos_ref[...]] * 2, axis=1)
    sinv = jnp.concatenate([-sin_ref[...], sin_ref[...]], axis=1)

    def rot(u):
        u = u.astype(F32)
        return (u * cosv + pltpu.roll(u, HD // 2, 1) * sinv).astype(BF16)

    for i in range(4):
        drain(wbuf.at[i], w_sem.at[i])
        acc = None
        for k in range(0, MODEL, KSTEP):
            ks = pl.ds(k, KSTEP)
            d = jnp.dot(xbuf[:, ks], wbuf[i, ks, :], preferred_element_type=F32)
            acc = d if acc is None else acc + d
        wo_copy(i).start()
        proj = acc.astype(BF16)
        for g in range(4):
            ro = rot(proj[:, g * HD:(g + 1) * HD])
            for tau in range(2):
                qsend[i, tau, g * TOK:(g + 1) * TOK, :] = ro[tau * TOK:(tau + 1) * TOK]
        kn = rot(proj[:, GRP:GRP + HD])
        vn = proj[:, GRP + HD:]
        for tau in range(2):
            rows = slice(tau * TOK, (tau + 1) * TOK)
            nsend[i, tau, :TOK, :] = kn[rows]
            nsend[i, tau, TOK:, :] = vn[rows]

        def keep_q(tau):
            qbuf[tau, here] = qsend[i, tau]

        def keep_n(tau):
            newbuf[0, 0] = nsend[i, tau]

        for tau in range(2):
            for ss in range(2):
                unless(q_dst(i, ss, tau) == me, lambda: q_copy(i, ss, tau).start(), lambda: keep_q(tau))
            unless(n_dst(i)[0] + tau == me, lambda: n_copy(i, tau).start(), lambda: keep_n(tau))
        for p in ((), (1, 2), (3,), ())[i]:
            stage1_arrive(p)

    def transpose_q(tau, zq):
        for yq in range(4):
            qt[tau * 4 + zq, :, yq * HD:(yq + 1) * HD] = qbuf[tau, zq * 4 + yq].T

    for zq in range(4):
        rows = pl.ds(zq * 4, 4)
        unless(jnp.logical_and(zq == z, c == src_core),
               lambda: drain(qbuf.at[c, rows], q_r.at[zq]),
               lambda: drain(qbuf.at[c, pl.ds(zq * 4, 3)], q_r.at[zq]))
        rcopy(qbuf.at[c, rows], qbuf.at[c, rows], qd_s, qd_r.at[zq], mate).start()
        transpose_q(c, zq)

    unless(c == src_core, lambda: drain(newbuf.at[0], n_r), lambda: drain(newbuf.at[0, pl.ds(1, HEADS - 1)], n_r))
    for k, xx in enumerate((xr, xl, xo)):
        rcopy(newbuf.at[0], newbuf.at[k + 1], nx_s, nx_r, dev(xx, y, z, c)).start()

    for p in range(4, HEADS):
        stage1_send(p)

    for zq in range(4):
        drain(qbuf.at[nc, pl.ds(zq * 4, 4)], qd_r.at[zq])
        transpose_q(nc, zq)

    def fold(op, v):
        return op(v.reshape(RC // SUB, SUB, QB), axis=0)

    def spread(v):
        return v.reshape(-1, SUB, QB)

    def q_pos(qb):
        lane = lax.broadcasted_iota(jnp.int32, (SUB, QB), 1)
        return rel_pos(dev(x, lane // HD, lax.rem(qb, 4), qb // 4), lax.rem(lane, TOK))

    def score_chunk(par, ref, qb, ch, mx, masked):
        sc = jnp.dot(ref[ch, KROWS, :], qt[qb], preferred_element_type=F32)
        if masked:
            kp = spread(jnp.concatenate([kpos[ch]] * (QB // HD), axis=1))
            sc = jnp.where(kp <= q_pos(qb)[None], spread(sc), -jnp.inf).reshape(RC, QB)
        sbuf[par, pl.ds(ch * RC, RC), :] = sc
        f = fold(jnp.max, sc)
        return f if mx is None else jnp.maximum(mx, f)

    def scores(par, ref, qb, masked=False):
        mx = None
        for ch in range(ref.shape[0]):
            mx = score_chunk(par, ref, qb, ch, mx, masked)
        return mx

    def step(par, mx, ref, qb, nref, nqb, masked=False):
        m_old = accs[qb, MROW, :]
        mn = jnp.maximum(m_old, jnp.broadcast_to(jnp.max(mx, axis=0, keepdims=True), (SUB, QB)))
        a = jnp.exp2((m_old - mn) * SCALE2)
        mx2 = ls = pv = None
        for ch in range(ref.shape[0]):
            mx2 = score_chunk(1 - par, nref, nqb, ch, mx2, masked)
            p = jnp.exp2((spread(sbuf[par, pl.ds(ch * RC, RC), :]) - mn[None]) * SCALE2)
            f = jnp.sum(p, axis=0)
            ls = f if ls is None else ls + f
            vt = jnp.concatenate([ref[ch, VLO, :], ref[ch, VHI, :]], axis=1)
            d = jnp.dot(vt, p.reshape(RC, QB).astype(BF16), preferred_element_type=F32)
            pv = d if pv is None else pv + d
        accs[qb, ACC, :] = (spread(accs[qb, ACC, :]) * a[None]).reshape(HD, QB) + pv
        accs[qb, MROW, :] = mn
        accs[qb, LROW, :] = accs[qb, LROW, :] * a + ls
        return mx2

    def tile_pass(ref, masked=False, beside=()):
        def body(it, mx):
            qb = 2 * it
            mx = step(0, mx, ref, qb, ref, qb + 1, masked)
            mx = step(1, mx, ref, qb + 1, ref, lax.rem(qb + 2, HEADS), masked)
            for k, run in enumerate(beside):
                pl.when(it == k)(run)
            return mx

        lax.fori_loop(0, HEADS // 2, body, scores(0, ref, 0, masked))

    def ring_pass(src, half):
        ring_wait(src, half)
        for p in range(2):
            forward(src, 4 * half + 2 * src - 2 + p)

    ring_pass(1, 0)

    def arrive(*ps):
        def run():
            for p in ps:
                stage1_arrive(p)
        return run

    tile_pass(kvt.at[0], beside=(lambda: ring_pass(2, 0), arrive(4), arrive(5), arrive(6, 7)))

    drain(newbuf.at[pl.ds(1, 3)], nx_r)
    for xs in range(4):
        for r in range(HEADS):
            kvn[xs, r * TOK:(r + 1) * TOK, :] = newbuf[xs, r, :TOK, :]
        for hf in range(2):
            vblk = jnp.concatenate([newbuf[xs, hf * 4 + r, TOK:, :] for r in range(4)], axis=0)
            kvn[xs, (VLO, VHI)[hf], :] = vblk.T

    tile_pass(kvn, True)

    ring_wait(3, 0)

    def blk(u):
        cc = jnp.where(lax.rem(u // 2, 2) == 0, nc, c)
        return 4 * jnp.where(u < 4, 1 - s, s) + 2 * cc + lax.rem(u, 2)

    def cc_copy(k):
        return rcopy(accs.at[blk(k + k // 2 * 2)], cb_core.at[k], cc_s, cc_r.at[k], mate)

    y_mate = dev(x, 2 * half_b + 1 - s, z, c)

    def cy_copy(k):
        return rcopy(accs.at[blk(k + 2)], cb_y.at[k], cy_s, cy_r.at[k], y_mate)

    def merge(dst, src):
        m0, m1 = accs[dst, MROW, :], src[MROW, :]
        mn = jnp.maximum(m0, m1)
        e0, e1 = jnp.exp2((m0 - mn) * SCALE2), jnp.exp2((m1 - mn) * SCALE2)
        accs[dst, ACC, :] = (spread(accs[dst, ACC, :]) * e0[None] + spread(src[ACC, :]) * e1[None]).reshape(HD, QB)
        accs[dst, MROW, :] = mn
        accs[dst, LROW, :] = accs[dst, LROW, :] * e0 + src[LROW, :] * e1

    def tail(it, mx):
        @pl.when(it == 1)
        def _():
            ring_pass(1, 1)
            ring_pass(2, 1)

        pl.when(it == 4)(lambda: ring_wait(3, 1))

        def at(i):
            return jnp.bitwise_and(TILES >> (2 * i), 3), 2 * jnp.bitwise_and(BLOCKS >> (2 * i), 3)

        k0, u0 = at(it)
        k1, u1 = at(jnp.minimum(it + 1, 11))
        mx = step(0, mx, kvt.at[k0], blk(u0), kvt.at[k0], blk(u0 + 1))
        mx = step(1, mx, kvt.at[k0], blk(u0 + 1), kvt.at[k1], blk(u1))

        @pl.when(it == 5)
        def _():
            cc_copy(0).start()
            cc_copy(1).start()

        @pl.when(it == 6)
        def _():
            for k in range(2):
                cc_copy(k).wait_recv()
                merge(blk(2 + k), cb_core.at[k])
                cy_copy(k).start()

        @pl.when(it == 9)
        def _():
            cc_copy(2).start()
            cc_copy(3).start()
        return mx

    lax.fori_loop(0, 12, tail, scores(0, kvt.at[1], blk(0)))

    def o_dst(e, yq):
        return dev(x, yq, 2 * c + e, s)

    def o_copy(e, yq):
        return rcopy(osend.at[e, yq], obuf.at[s, head], o_s, o_r.at[head], o_dst(e, yq))

    def keep_o(e, yq):
        obuf[s, head] = osend[e, yq]

    for e in range(2):
        b = blk(jnp.int32(HEADS - 2 + e))
        cc_copy(2 + e).wait_recv()
        merge(b, cb_core.at[2 + e])
        cy_copy(e).wait_recv()
        merge(b, cb_y.at[e])
        o = accs[b, ACC, :] / jnp.sum(accs[b, LROW, :], axis=0, keepdims=True)
        for yq in range(4):
            osend[e, yq] = o[:, yq * HD:(yq + 1) * HD].T.astype(BF16)
            unless(o_dst(e, yq) == me, lambda: o_copy(e, yq).start(), lambda: keep_o(e, yq))

    def od_copy(h):
        return rcopy(obuf.at[c, h], obuf.at[c, h], od_s, od_r, mate)

    for h in range(HEADS):
        src = dev(x, 2 * (h % 2) + c, h // 2, z // 2)
        unless(src == me, lambda: drain(obuf.at[c, h], o_r.at[h]))
        od_copy(h).start()

    def spread_o(tok, tau):
        for h in range(HEADS):
            for g in range(4):
                col = (h * 4 + g) * HD
                olhs[tok, col:col + HD] = obuf[tau, h, g * TOK:(g + 1) * TOK, :]

    spread_o(my_tok, c)
    drain(obuf.at[nc], od_r)
    spread_o(mate_tok, nc)

    def y_copy(n):
        cols = pl.ds(n * WCOLS, OTILES[n])
        dst = pl.ds(pl.multiple_of(c * OHALF, HD) + n * WCOLS, OTILES[n])
        return rcopy(ysend.at[mate_tok, cols], ybuf.at[:, dst], y_s, y_r, mate)

    for n in range(4):
        wide = OTILES[n]
        wo_copy(n).wait()
        acc = None
        for k in range(0, QCOLS, OSTEP):
            ks = pl.ds(k, OSTEP)
            d = jnp.dot(olhs[:, ks], wbuf[n, ks, :wide], preferred_element_type=F32)
            acc = d if acc is None else acc + d
        cols = pl.ds(n * WCOLS, wide)
        dst = pl.ds(pl.multiple_of(c * OHALF, HD) + n * WCOLS, wide)
        ysend[:, cols] = (xbuf[:, dst].astype(F32) + acc).astype(BF16)
        y_copy(n).start()
        ybuf[:, dst] = ysend[my_tok, cols]
    drain(ysend.at[my_tok], y_r)
    fin = pltpu.make_async_copy(ybuf, out_hbm, loc_sem.at[0])
    fin.start()

    x_ex.wait_send()
    drain(kvt.at[0, pl.ds(0, HEADS - 1)], kv1_s)
    drain(kvt.at[pl.ds(0, 3)], kvx_s)
    q_kept = c == src_core
    all_q = qbuf.at[0]
    unless(q_kept, lambda: drain(all_q, q_s), lambda: drain(qbuf.at[0, pl.ds(0, 15)], q_s))
    unless(q_kept, lambda: drain(newbuf.at[0], n_s), lambda: drain(newbuf.at[0, pl.ds(0, HEADS - 1)], n_s))
    drain(all_q, qd_s)
    drain(newbuf.at[pl.ds(0, 3)], nx_s)
    drain(cb_core, cc_s)
    drain(cb_y, cy_s)
    o_kept = jnp.logical_and(s == c, z // 2 == c)
    unless(o_kept, lambda: drain(obuf.at[0], o_s), lambda: drain(obuf.at[0, pl.ds(0, HEADS - 1)], o_s))
    drain(obuf.at[0], od_s)
    drain(ysend.at[mate_tok], y_s)
    fin.wait()


def solution(mesh):
    def local_step(x_loc, pos_loc, k_loc, v_loc, w_q, w_k, w_v, w_o):
        me = lax.axis_index("cp")
        p0 = pos_loc[0] - HALF * me
        row = jnp.arange(PAIR, dtype=jnp.int32)
        pos = p0 + rel_pos((me // 2) * 2 + row // TOK, row % TOK)
        inv_freq = jnp.power(F32(ROPE_BASE), -(jnp.arange(HD // 2, dtype=F32) * 2.0 / HD))
        ang = pos.astype(F32)[:, None] * inv_freq[None, :]
        vm = pltpu.VMEM
        anyspec = pl.BlockSpec(memory_space=pl.ANY)
        vspec = pl.BlockSpec(memory_space=pltpu.VMEM)
        one = ()
        dmas = ((3,), (8,), (2,), one, (8,), one, (4, 2), one, (4,), one, (4,),
                one, one, one, one, one, (4,), one, (2,), one, (8,), one, one, one, one)
        return pl.pallas_call(
            kernel,
            out_shape=jax.ShapeDtypeStruct((TOK, MODEL), BF16),
            in_specs=[anyspec, anyspec, anyspec, vspec, vspec, anyspec, anyspec, anyspec, anyspec],
            out_specs=anyspec,
            scratch_shapes=[
                vm((PAIR, MODEL), BF16),
                vm((2, CACHE, HEADS, HD), BF16),
                vm((HEADS, 2 * CACHE, HD), BF16),
                vm((4, 8, 2 * CACHE, HD), BF16),
                vm((4, 2 * CACHE, HD), BF16),
                vm((4, 8, PAIR, HD), BF16),
                vm((2, 16, HD, HD), BF16),
                vm((HEADS, HD, QB), BF16),
                vm((4, 2, HD, HD), BF16),
                vm((4, 2, PAIR, HD), BF16),
                vm((HEADS, STAT, QB), F32),
                vm((4, STAT, QB), F32),
                vm((2, STAT, QB), F32),
                vm((2, KT, QB), F32),
                vm((4, MODEL, WCOLS), BF16),
                vm((2, 4, HD, HD), BF16),
                vm((2, HEADS, HD, HD), BF16),
                vm((PAIR, QCOLS), BF16),
                vm((4, RC, HD), jnp.int32),
                vm((PAIR, OHALF), BF16),
                vm((TOK, MODEL), BF16),
            ] + [pltpu.SemaphoreType.DMA(n) for n in dmas],
            compiler_params=pltpu.CompilerParams(
                collective_id=0, has_side_effects=True, vmem_limit_bytes=67043328),
        )(x_loc, k_loc, v_loc, jnp.cos(ang), jnp.sin(ang), w_q, w_k, w_v, w_o)

    tok_spec = P(("data", "cp"), None)
    pos_spec = P(("data", "cp"))
    cache_spec = P(("data", "cp"), None, None)
    return jax.shard_map(local_step, mesh=mesh, in_specs=(tok_spec, pos_spec, cache_spec, cache_spec, P(), P(), P(), P()), out_specs=tok_spec, check_vma=False)
```

time: 1890 us -> 100 us (0.05)
  the two profiles are of different devices: /device:TPU:117 before, /device:TPU:32 now
where the time goes in v1:
time: 100 us
  Pallas kernels  96.8 us (97%)
  local copies, waits for them, and re-layouts  1.72 us (2%)
    pallas_call x1, Pallas kernels, local_step(): pl.pallas_call(kernel, out_shape=jax.ShapeDtypeStruct((TOK, MODEL), BF16)...  96.8 us

profile of v1, /device:TPU:32, one launch (start us, length us, event | category | flops | bytes accessed | tf_op | source)
XLA Modules:
  0.0 100.0 jit_solution(12631099271236953823)
XLA Ops:
  0.7 0.8 multiply_sine_fusion
  1.5 96.8 %shard_map.82 = bf16[32,5120]{1,0:T(8,128)(2,1)} custom-call(bf16[32,5120]{1,0:T(8,128)(2,1)} %x_hbm.1, bf16[256,8,128]{2,1,0:T(8,128)(2,1)} %k_hbm.1, bf16[256,8,128]{2,1,0:T(8,128)(2,1)} %v_hbm.1, f32[64,64]{1,0:T(8,128)} %get-tuple-element.6.cos_ref, f32[64,64]{1,0:T(8,128)} %get-tuple-element.5.sin_ref, bf16[5120,4096]{1,0:T(8,128)(2,1)} %wq.1, ...), custom_call_target="tpu_custom_call" | custom-call | tf_op jit(solution)/shard_map/pallas_call | solution.py:500
  98.3 1.7 %copy.10 = bf16[32,5120]{1,0:T(8,128)(2,1)} copy(bf16[32,5120]{1,0:T(8,128)(2,1)} %shard_map.82) | data formatting | bytes 655360
  (2 shorter events, 0.0 us)
